TPU v7x, 32 devices: a whole 2x2x4 slice. The times are simulated.
32 devices in a mesh: dp: 2 (over x), vocab: 16 (over z, y, core).
Axes of the slice: x: 2, y: 2, z: 4, core: 2. Of those that a mesh axis runs over, the one named last changes fastest.
Arguments:
- hidden: bfloat16 [1536, 4096], P(('dp', 'vocab')), may hold values from -75 to 75
- embedding: bfloat16 [8192, 4096], P(('dp', 'vocab')), may hold values from -0.5 to 0.5
- targets: int32 [1536], replicated, may hold values from 0 to 8191
Outputs:
- token_loss: float32 [1536], P(('dp', 'vocab'))
- mean_loss: float32 [], replicated
All inputs are finite; a program needn't handle non-finite values.
Results may differ from a plain program's by a relative error of at most 0.00055.
Values may be sent and summed in bfloat16 or wider, within the bound.
No kernel may reach another device: no remote copies, remote signals or barrier semaphores. Data moves between devices by JAX's collectives and lax.ppermute only.
A program may use at most 64 MiB of HBM per device.

v0:
```python
import jax
import jax.numpy as jnp
from jax import lax
from jax.sharding import PartitionSpec as P


def picked_of(logits, wanted, global_ids):
    matches = wanted[:, None] == global_ids[None, :]
    return jnp.sum(jnp.where(matches, logits, jnp.zeros_like(logits)), axis=1)


def scores(left_rows, right_rows):
    return lax.dot_general(
        left_rows, right_rows, (((1,), (1,)), ((), ())), preferred_element_type=jnp.float32
    )


def local(hidden, embedding, targets):
    vocab_count = lax.axis_size("vocab")
    vocab_index = lax.axis_index("vocab")
    group_index = lax.axis_index("dp")
    tok_dev = hidden.shape[0]
    shard_rows = embedding.shape[0]
    device_index = group_index * vocab_count + vocab_index
    global_ids = device_index * shard_rows + jnp.arange(shard_rows, dtype=jnp.int32)
    logits = scores(lax.all_gather(hidden, ("dp", "vocab"), axis=0, tiled=True), embedding)
    maxima = lax.pmax(jnp.max(logits, axis=1), ("dp", "vocab"))
    local_totals = jnp.sum(jnp.exp(logits - maxima[:, None]), axis=1)
    local_picked = picked_of(logits, targets, global_ids)
    totals, picked = lax.psum((local_totals, local_picked), ("dp", "vocab"))
    losses = maxima + jnp.log(totals) - picked
    mean_loss = jnp.sum(losses) / losses.shape[0]
    token_loss = lax.dynamic_slice_in_dim(losses, device_index * tok_dev, tok_dev)
    return (token_loss, mean_loss)


def solution(mesh):
    return jax.shard_map(
        local,
        mesh=mesh,
        in_specs=(P(("dp", "vocab"), None), P(("dp", "vocab"), None), P()),
        out_specs=(P(("dp", "vocab")), P()),
        check_vma=False,
    )
```

profile of v0, /device:TPU:0, one launch (start us, length us, event | category | flops | bytes accessed | tf_op | source)
XLA Modules:
  0.0 207.5 jit_solution(15314080642424589533)
XLA Ops:
  7.2 0.0 copy-start
  7.2 0.0 all-gather.2.cloned.1.call-start
  7.2 0.7 all-gather.2.cloned.1.call-update
  7.9 0.0 copy-start.1
  7.9 100.9 %all-gather.2.cloned.1.call-done = bf16[1536,4096]{1,0:T(8,128)(2,1)} async-done(((bf16[48,4096]{1,0:T(8,128)(2,1)}), bf16[1536,4096]{1,0:T(8,128)(2,1)}) %all-gather.2.cloned.1.call-update) | async-done | bytes 12582928 | tf_op jit(solution)/shard_map/all_gather | solution.py:26
  108.8 0.0 copy-done
  108.8 7.7 %fusion.1 = (f32[1536]{0:T(1024)S(1)}, f32[1536,256]{0,1:T(8,128)}) fusion(bf16[1536,4096]{1,0:T(8,128)(2,1)} %all-gather.2.cloned.1.call-done, bf16[256,4096]{1,0:T(8,128)(2,1)S(1)} %copy-done), kind=kOutput, calls=%fused_computation.5 | convolution fusion | flops 3221617152 | bytes 16259072 | tf_op jit(solution)/shard_map/dot_general | solution.py:13
  116.5 38.9 %pmax.7 = f32[1536]{0:T(1024)S(1)} all-reduce(f32[1536]{0:T(1024)S(1)} %get-tuple-element.8), channel_id=1, replica_groups=mesh['dp'=2,'vocab'=16] {'dp','vocab'}, use_global_device_ids=true, to_apply=%region_1.0 | all-reduce | flops 1536 | bytes 12288 | tf_op jit(solution)/shard_map/pmax | solution.py:27
  155.5 0.0 copy-done.1
  155.5 1.8 exponential_reduce_fusion
  157.3 40.4 %all-reduce = (f32[1536]{0:T(1024)S(1)}, f32[1536]{0:T(1024)S(1)}) all-reduce(f32[1536]{0:T(1024)S(1)} %get-tuple-element.3, f32[1536]{0:T(1024)S(1)} %get-tuple-element.2), channel_id=1, replica_groups=mesh['dp'=2,'vocab'=16] {'dp','vocab'}, use_global_device_ids=true, to_apply=%region_5.6 | all-reduce | flops 3072 | bytes 24576 | tf_op jit(solution)/shard_map/psum | solution.py:30
  197.7 0.6 fusion
  198.3 0.6 dynamic_slice.3
  (1 shorter events, 0.0 us)
Async XLA Ops:
  7.2 101.7 %copy-start = (bf16[256,4096]{1,0:T(8,128)(2,1)S(1)}, bf16[256,4096]{1,0:T(8,128)(2,1)}, u32[]{:S(2)}) copy-start(bf16[256,4096]{1,0:T(8,128)(2,1)} %param.4) | copy-start | bytes 6291460
  7.2 101.6 %all-gather.2.cloned.1.call-start = ((), (), s32[]{:S(2)}) async-start(), calls=%async_computation | async-start | bytes 12976128 | tf_op jit(solution)/shard_map/all_gather | solution.py:26
  7.9 147.5 %copy-start.1 = (s32[1536]{0:T(1024)S(1)}, s32[1536]{0:T(1024)}, u32[]{:S(2)}) copy-start(s32[1536]{0:T(1024)} %param.5) | copy-start | bytes 18436
Sparse Core Ops, SparseCore 0:
  10.9 97.8 all-gather.1
where the time goes:
time: 208 us; the launch traced here: 207 us
  waiting for transfers between devices  102 us (49%)
  blocking collectives  79.3 us (38%)
  between operations  15.8 us (8%)
  matrix products  7.73 us (4%)
  other arithmetic  2.41 us (1%)
    all_gather x1, waiting for transfers between devices, local(): lax.all_gather(hidden, ('dp', 'vocab'), axis=0, tiled=True)  101 us
    psum x1, blocking collectives, local(): totals, picked = lax.psum((local_totals, local_picked), ('dp', 'vocab'))  40.4 us
    pmax x1, blocking collectives, local(): maxima = lax.pmax(jnp.max(logits, axis=1), ('dp', 'vocab'))  38.9 us
    dot_general x1, matrix products, scores(): lax.dot_general(left_rows, right_rows, (((1,), (1,)), ((), ())), preferre...  7.73 us
  transfers between devices with their start and end apart: 1, of which 1 were waited for; matrix products, arithmetic and copies ran while one was open for 0% of the time, Pallas kernels for 0%

commit v1 on v0

--- a/solution.py
+++ b/solution.py
@@ -27,7 +27,7 @@
     maxima = lax.pmax(jnp.max(logits, axis=1), ("dp", "vocab"))
     local_totals = jnp.sum(jnp.exp(logits - maxima[:, None]), axis=1)
     local_picked = picked_of(logits, targets, global_ids)
-    totals, picked = lax.psum((local_totals, local_picked), ("dp", "vocab"))
+    totals, picked = lax.psum(lax.psum((local_totals, local_picked), "vocab"), "dp")
     losses = maxima + jnp.log(totals) - picked
     mean_loss = jnp.sum(losses) / losses.shape[0]
     token_loss = lax.dynamic_slice_in_dim(losses, device_index * tok_dev, tok_dev)

time: 208 us -> 234 us (1.12)
  blocking collectives: 79.3 us -> 106 us
    psum x1 -> x2, blocking collectives: 40.4 us -> 67 us  [the longest x1 60 us: local(): lax.psum((local_totals, local_picked), 'vocab')]
where the time goes in v1:
time: 234 us
  blocking collectives  106 us (45%)
  waiting for transfers between devices  102 us (44%)
  between operations  15.8 us (7%)
  matrix products  7.73 us (3%)
  other arithmetic  2.41 us (1%)
    all_gather x1, waiting for transfers between devices, local(): lax.all_gather(hidden, ('dp', 'vocab'), axis=0, tiled=True)  101 us
    psum x1, blocking collectives, local(): lax.psum((local_totals, local_picked), 'vocab')  60 us
    pmax x1, blocking collectives, local(): maxima = lax.pmax(jnp.max(logits, axis=1), ('dp', 'vocab'))  38.9 us
    dot_general x1, matrix products, scores(): lax.dot_general(left_rows, right_rows, (((1,), (1,)), ((), ())), preferre...  7.73 us
    psum x1, blocking collectives, local(): lax.psum(lax.psum((local_totals, local_picked), 'vocab'), 'dp')  7.03 us
  transfers between devices with their start and end apart: 1, of which 1 were waited for; matrix products, arithmetic and copies ran while one was open for 0% of the time, Pallas kernels for 0%

profile of v1, /device:TPU:0, one launch (start us, length us, event | category | flops | bytes accessed | tf_op | source)
XLA Modules:
  0.0 234.1 jit_solution(13107249898507563873)
XLA Ops:
  7.2 0.0 copy-start
  7.2 0.0 all-gather.2.cloned.1.call-start
  7.2 0.7 all-gather.2.cloned.1.call-update
  7.9 0.0 copy-start.1
  7.9 100.9 %all-gather.2.cloned.1.call-done = bf16[1536,4096]{1,0:T(8,128)(2,1)} async-done(((bf16[48,4096]{1,0:T(8,128)(2,1)}), bf16[1536,4096]{1,0:T(8,128)(2,1)}) %all-gather.2.cloned.1.call-update) | async-done | bytes 12582928 | tf_op jit(solution)/shard_map/all_gather | solution.py:26
  108.8 0.0 copy-done
  108.8 7.7 %fusion.1 = (f32[1536]{0:T(1024)S(1)}, f32[1536,256]{0,1:T(8,128)}) fusion(bf16[1536,4096]{1,0:T(8,128)(2,1)} %all-gather.2.cloned.1.call-done, bf16[256,4096]{1,0:T(8,128)(2,1)S(1)} %copy-done), kind=kOutput, calls=%fused_computation.5 | convolution fusion | flops 3221617152 | bytes 16259072 | tf_op jit(solution)/shard_map/dot_general | solution.py:13
  116.5 38.9 %pmax.7 = f32[1536]{0:T(1024)S(1)} all-reduce(f32[1536]{0:T(1024)S(1)} %get-tuple-element.10), channel_id=1, replica_groups=mesh['dp'=2,'vocab'=16] {'dp','vocab'}, use_global_device_ids=true, to_apply=%region_1.0 | all-reduce | flops 1536 | bytes 12288 | tf_op jit(solution)/shard_map/pmax | solution.py:27
  155.5 0.0 copy-done.1
  155.5 1.8 exponential_reduce_fusion
  157.3 60.0 %all-reduce = (f32[1536]{0:T(1024)S(1)}, f32[1536]{0:T(1024)S(1)}) all-reduce(f32[1536]{0:T(1024)S(1)} %get-tuple-element.3, f32[1536]{0:T(1024)S(1)} %get-tuple-element.2), channel_id=1, replica_groups=mesh['dp'=2,'vocab'=16] {'vocab'}, use_global_device_ids=true, to_apply=%region_6.7 | all-reduce | flops 3072 | bytes 24576 | tf_op jit(solution)/shard_map/psum | solution.py:30
  217.3 7.0 %all-reduce.1 = (f32[1536]{0:T(1024)S(1)}, f32[1536]{0:T(1024)S(1)}) all-reduce(f32[1536]{0:T(1024)S(1)} %get-tuple-element.4, f32[1536]{0:T(1024)S(1)} %get-tuple-element.5), channel_id=1, replica_groups=mesh['dp'=2,'vocab'=16] {'dp'}, use_global_device_ids=true, to_apply=%region_7.8 | all-reduce | flops 3072 | bytes 24576 | tf_op jit(solution)/shard_map/psum | solution.py:30
  224.3 0.6 fusion
  224.9 0.6 dynamic_slice.3
  (1 shorter events, 0.0 us)
Async XLA Ops:
  7.2 101.7 %copy-start = (bf16[256,4096]{1,0:T(8,128)(2,1)S(1)}, bf16[256,4096]{1,0:T(8,128)(2,1)}, u32[]{:S(2)}) copy-start(bf16[256,4096]{1,0:T(8,128)(2,1)} %param.4) | copy-start | bytes 6291460
  7.2 101.6 %all-gather.2.cloned.1.call-start = ((), (), s32[]{:S(2)}) async-start(), calls=%async_computation | async-start | bytes 12976128 | tf_op jit(solution)/shard_map/all_gather | solution.py:26
  7.9 147.5 %copy-start.1 = (s32[1536]{0:T(1024)S(1)}, s32[1536]{0:T(1024)}, u32[]{:S(2)}) copy-start(s32[1536]{0:T(1024)} %param.5) | copy-start | bytes 18436
Sparse Core Ops, SparseCore 0:
  10.9 97.8 all-gather.1
